TPU v7x, 32 devices: a 4x4x1 block of a 4x4x8 slice. The times are simulated.
32 devices in a mesh: dp: 1 (over z), tp: 32 (over y, x, core).
Axes of the slice: x: 4, y: 4, z: 1, core: 2. Of those that a mesh axis runs over, the one named last changes fastest.
The devices are a block of a 4x4x8 slice.
Arguments:
- resid_in: bfloat16 [512, 2048], P('dp')
- cand_ids: int32 [512, 256], P('dp')
- ln_mlp: bfloat16 [2048], replicated
- wi_gate: bfloat16 [2048, 5120], P(None, 'tp')
- wi_lin: bfloat16 [2048, 5120], P(None, 'tp')
- w_out: bfloat16 [5120, 2048], P('tp')
- ln_final: bfloat16 [2048], replicated
- w_lm: bfloat16 [2048, 256384], P(None, 'tp')
Outputs:
- output 1: float32 [512, 256], P('dp')
- output 2: float32 [512], P('dp')
All inputs are finite; a program needn't handle non-finite values.
Results may differ from a plain program's by a relative error of at most 0.00164064.
Values sent between devices are 32-bit elements.
A program may use at most 768 MiB of HBM per device.

v0:
```python
import jax
import jax.numpy as jnp
from jax import lax
from jax.sharding import PartitionSpec as P

EPS = 1e-6


def rms_norm(values_in, scale_vec):
    wide = values_in.astype(jnp.float32)
    mean_sq = jnp.mean(wide * wide, axis=-1, keepdims=True)
    return (wide * lax.rsqrt(mean_sq + EPS) * scale_vec.astype(jnp.float32)).astype(jnp.bfloat16)


def solution(mesh):
    def local_step(resid_in, cand_ids, ln_mlp, wi_gate, wi_lin, w_out, ln_final, w_lm):
        normed = rms_norm(resid_in, ln_mlp)
        act_gate = jnp.dot(normed, wi_gate, preferred_element_type=jnp.float32)
        act_lin = jnp.dot(normed, wi_lin, preferred_element_type=jnp.float32)
        hidden = (jax.nn.gelu(act_gate, approximate=True) * act_lin).astype(jnp.bfloat16)
        part_out = jnp.dot(hidden, w_out, preferred_element_type=jnp.float32)
        mlp_out = lax.psum(part_out, "tp")
        resid_out = (resid_in.astype(jnp.float32) + mlp_out).astype(jnp.bfloat16)
        final_z = rms_norm(resid_out, ln_final)
        logits = jnp.dot(final_z, w_lm, preferred_element_type=jnp.float32)
        shard_cols = logits.shape[1]
        row_max = lax.pmax(jnp.max(logits, axis=-1), "tp")
        exp_sum = lax.psum(jnp.sum(jnp.exp(logits - row_max[:, None]), axis=-1), "tp")
        log_norm = row_max + jnp.log(exp_sum)
        local_ids = cand_ids - lax.axis_index("tp") * shard_cols
        is_owned = (local_ids >= 0) & (local_ids < shard_cols)
        picked = jnp.take_along_axis(logits, jnp.clip(local_ids, 0, shard_cols - 1), axis=1)
        cand_logits = lax.psum(jnp.where(is_owned, picked, 0.0), "tp")
        return cand_logits - log_norm[:, None], log_norm

    in_specs = (P("dp", None), P("dp", None), P(None), P(None, "tp"), P(None, "tp"), P("tp", None), P(None), P(None, "tp"))
    return jax.shard_map(local_step, mesh=mesh, in_specs=in_specs, out_specs=(P("dp", None), P("dp")), check_vma=False)
```

profile of v0, /device:TPU:97, one launch (start us, length us, event | category | flops | bytes accessed | tf_op | source)
XLA Modules:
  0.0 5975.2 jit_solution(8032779330028235348)
XLA Ops:
  7.2 0.0 copy-start
  7.2 0.0 copy-start.1
  7.2 0.1 all-reduce.3.cloned.1.call-start
  7.3 0.8 convert_element_type.26
  8.1 2.1 fusion.3
  10.2 3.4 fusion.24
  13.6 0.0 copy-done
  13.6 0.0 copy-done.1
  13.6 0.0 copy-start.7
  13.6 0.0 copy-start.3
  13.6 4.7 fusion.12
  18.4 0.1 all-reduce.3.cloned.1.call-update
  18.4 0.1 all-reduce.5.cloned.1.call-start
  18.5 0.0 copy-done.7
  18.5 0.0 copy-done.3
  18.5 0.3 fusion.17
  18.8 0.3 copy.10
  19.1 104.6 %all-reduce.3.cloned.1.call-done = f32[512,2048]{1,0:T(8,128)} async-done(((f32[512,2048]{1,0:T(8,128)}), f32[512,2048]{1,0:T(8,128)}) %all-reduce.3.cloned.1.call-update) | async-done | bytes 4194320 | tf_op jit(solution)/shard_map/psum | solution.py:22
  123.7 0.0 copy-start.2
  123.7 3.0 fusion
  126.6 0.5 copy-done.2
  127.1 25.1 fusion.28
  152.2 45.6 pmax.7
  197.8 0.0 copy-start.4
  197.8 0.0 copy-start.5
  197.8 3582.0 %gather_fusion = f32[131072]{0:T(1024)S(1)} fusion(f32[512,8012]{0,1:T(8,128)} %get-tuple-element.3, s32[131072]{0:T(1024)S(1)} %bitcast.12), kind=kCustom, calls=%fused_computation | custom fusion | bytes 2097152 | tf_op jit(solution)/shard_map/jit(take_along_axis)/gather | solution.py:32
  3779.8 0.1 reshape.37
  3779.9 0.0 copy-done.4
  3779.9 1.1 select_select_fusion
  3781.0 0.1 all-reduce.5.cloned.1.call-update
  3781.1 0.0 copy-done.5
  3781.1 7.9 exponential_reduce_fusion
  3789.0 2138.2 %psum.23 = f32[512]{0:T(512)S(1)} all-reduce(f32[512]{0:T(512)S(1)} %exponential_reduce_fusion), channel_id=1, replica_groups=mesh['dp'=1,'tp'=32] {'tp'}, use_global_device_ids=true, to_apply=%region_7.8 | all-reduce | flops 512 | bytes 4096 | tf_op jit(solution)/shard_map/psum | solution.py:28
  5927.1 0.0 copy-start.6
  5927.1 39.2 all-reduce.5.cloned.1.call-done
  5966.4 2.0 broadcast_subtract_fusion
  5968.3 0.0 copy-done.6
  (4 shorter events, 0.0 us)
Async XLA Ops:
  7.2 6.4 copy-start
  7.2 6.4 copy-start.1
  7.2 116.5 %all-reduce.3.cloned.1.call-start = ((), (), s32[]{:S(2)}) async-start(), calls=%async_computation | async-start | bytes 8388608 | tf_op jit(solution)/shard_map/psum | solution.py:22
  13.6 4.9 copy-start.7
  13.6 4.9 copy-start.3
  18.4 5947.9 %all-reduce.5.cloned.1.call-start = ((), (), s32[]{:S(2)}) async-start(), calls=%async_computation.1 | async-start | bytes 1048576 | tf_op jit(solution)/shard_map/psum | solution.py:33
  123.7 3.4 copy-start.2
  197.8 3582.1 %copy-start.4 = (s32[512,256]{1,0:T(8,128)S(1)}, s32[512,256]{1,0:T(8,128)}, u32[]{:S(2)}) copy-start(s32[512,256]{1,0:T(8,128)} %param.9) | copy-start | bytes 1572868
  197.8 3583.3 %copy-start.5 = (f32[512]{0:T(512)S(1)}, f32[512]{0:T(512)}, u32[]{:S(2)}) copy-start(f32[512]{0:T(512)} %pmax.7) | copy-start | bytes 6148
  5927.1 41.2 copy-start.6
Sparse Core Ops, SparseCore 0:
  18.5 105.0 all-reduce.2
  3781.2 2185.1 all-reduce.4
where the time goes:
time: 6080 us; the launch traced here: 5980 us
  local copies, waits for them, and re-layouts  3580 us (59%)
  blocking collectives  2180 us (36%)
  waiting for transfers between devices  144 us (2%)
    gather x2, local copies, waits for them, and re-layouts, local_step(): jnp.take_along_axis(logits, jnp.clip(local_ids, 0, shard_cols - 1), axis=1)  3580 us
    psum x1, blocking collectives, local_step(): lax.psum(jnp.sum(jnp.exp(logits - row_max[:, None]), axis=-1), 'tp')  2140 us
  transfers between devices with their start and end apart: 2, of which 2 were waited for; matrix products, arithmetic and copies ran while one was open for 0% of the time, Pallas kernels for 0%

commit v1 on v0

v1 whole, which is shorter than its diff:
```python
import functools
import math

import jax
import jax.numpy as jnp
from jax import lax
from jax.experimental import pallas as pl
from jax.experimental.pallas import tpu as pltpu
from jax.sharding import PartitionSpec as P

EPS = 1e-6
LANES = 128
CORES = 2
MESH = pl.DeviceIdType.MESH
NEG = float("-inf")

NORTH = False
ROWS_LM = 128
TILE = 256


def rms_rows(wide, scale):
    mean_sq = jnp.mean(wide * wide, axis=-1, keepdims=True)
    return (wide * lax.rsqrt(mean_sq + EPS) * scale).astype(jnp.bfloat16)


def log_add(parts):
    top = functools.reduce(jnp.maximum, parts)
    total = functools.reduce(jnp.add, [jnp.exp(p - top) for p in parts])
    return top + jnp.log(total)


class Link:
    def __init__(self, src, dst, send, recv, to):
        self.args = dict(
            src_ref=src, dst_ref=dst, send_sem=send, recv_sem=recv,
            device_id={"tp": to}, device_id_type=MESH,
        )

    def make(self):
        return pltpu.make_async_remote_copy(**self.args)

    def start(self):
        self.make().start()

    def sent(self):
        self.make().wait_send()

    def came(self):
        self.make().wait_recv()


def fused(cfg, x_hbm, ids_hbm, lnm_ref, wg_hbm, wl_hbm, wo_hbm, lnf_ref, w_hbm,
          lp_hbm, ln_hbm,
          x_v, ids_v, wg_v, wl_v, wo_v, w_v, z_v, lg_v, st_v, lse_v, lnrow_v, ob_v,
          bufs, tails, send_sems, recv_sems, loc_sems):
    q, chunks, lm_chunks = cfg["q"], cfg["chunks"], cfg["lm"]
    me = lax.axis_index("tp")
    core = lax.rem(me, CORES)
    x = lax.rem(me // CORES, q)
    y = me // (CORES * q)
    sibling = me + 1 - 2 * core
    vocab = w_v.shape[1]
    ndev_side = q

    if NORTH:
        slots = [0, 1]
        half_of = [0, 1]
        speak = 1
    else:
        slots = [0]
        half_of = [core]
        speak = core

    def coords(s):
        if NORTH:
            return (x, y) if s == 0 else (y, x)
        a = jnp.where(core == 0, x, y)
        b = jnp.where(core == 0, y, x)
        return a, b

    def device(s, a, b):
        if NORTH:
            col, row = (a, b) if s == 0 else (b, a)
            return (row * q + col) * CORES + 1
        col = jnp.where(core == 0, a, b)
        row = jnp.where(core == 0, b, a)
        return (row * q + col) * CORES + core

    def step(v, d):
        return lax.rem(v + d + q, q)

    counter = [0]
    started = {"all": [], "talk": [], "quiet": []}

    def link(src, dst, to, who="talk"):
        i = counter[0]
        counter[0] += 1
        made = Link(src, dst, send_sems.at[i], recv_sems.at[i], to)
        started[who].append(made)
        return made

    def talkers(fn):
        if NORTH:
            pl.when(core == 1)(fn)
        else:
            fn()

    def quiet(fn):
        if NORTH:
            pl.when(core == 0)(fn)

    loads = {}
    loc_count = [0]

    def load(name, src, dst):
        i = loc_count[0]
        loc_count[0] += 1
        cp = pltpu.make_async_copy(src, dst, loc_sems.at[i])
        loads[name] = cp
        cp.start()

    off0, rows0 = chunks[0]
    load("x0", x_hbm.at[pl.ds(off0, rows0), :], x_v.at[pl.ds(off0, rows0), :])
    load("wg", wg_hbm, wg_v)
    load("wl", wl_hbm, wl_v)
    load("wo", wo_hbm, wo_v)
    for k, (off, rows) in enumerate(chunks[1:], 1):
        load(f"x{k}", x_hbm.at[pl.ds(off, rows), :], x_v.at[pl.ds(off, rows), :])
    load("ids", ids_hbm, ids_v)
    parts = cfg["w_parts"]
    depth = w_v.shape[0] // parts
    for i in range(parts):
        load(f"w{i}", w_hbm.at[pl.ds(i * depth, depth), :], w_v.at[pl.ds(i * depth, depth), :])

    barrier = pltpu.get_barrier_semaphore()

    def greet(to):
        pl.semaphore_signal(barrier, inc=1, device_id={"tp": to}, device_id_type=MESH)

    greet(sibling)

    def greet_far():
        a, b = coords(0)
        for d in range(1, q):
            greet(device(0, step(a, d), b))
            greet(device(0, a, step(b, d)))

    talkers(greet_far)

    def meet():
        if NORTH:
            pl.when(core == 1)(lambda: pl.semaphore_wait(barrier, 1 + 2 * (q - 1)))
            pl.when(core == 0)(lambda: pl.semaphore_wait(barrier, 1))
        else:
            pl.semaphore_wait(barrier, 1 + 2 * (q - 1))

    scale_mlp = lnm_ref[...].astype(jnp.float32)
    scale_fin = lnf_ref[...].astype(jnp.float32)

    plans = []
    for k, (off, rows) in enumerate(chunks):
        r2 = rows // 2
        hr = r2 // 2
        px, dr, rl, dc, cb, bs, pr, xb = bufs[k]
        plan = {"slots": []}
        if NORTH:
            plan["pair"] = [link(px.at[h], dr.at[h], sibling, "quiet") for h in (0, 1)]
        else:
            plan["pair"] = [link(px.at[1 - core], dr.at[0], sibling)]
        for s in slots:
            a, b = coords(s)
            h = half_of[s]
            up, down, far = step(a, 1), step(a, -1), step(a, 2)
            to_up, to_down = device(s, up, b), device(s, down, b)
            lo, hi = pl.ds(0, hr), pl.ds(hr, hr)

            def grp(v):
                return pl.ds(v * q, q)

            e = {}
            e["relay"] = [
                link(dr.at[s, grp(far), lo, :], rl.at[s, 0], to_up),
                link(dr.at[s, grp(far), hi, :], rl.at[s, 1], to_down),
            ]
            e["direct"] = [
                link(dr.at[s, grp(down), lo, :], dc.at[s, 0], to_down),
                link(dr.at[s, grp(up), hi, :], dc.at[s, 1], to_up),
            ]
            e["comb"] = [
                link(rl.at[s, 0], cb.at[s, 0], to_up),
                link(rl.at[s, 1], cb.at[s, 1], to_down),
            ]
            e["second"] = [
                link(bs.at[s, step(b, d)], pr.at[s, d - 1], device(s, a, step(b, d)))
                for d in range(1, q)
            ]
            own = xb.at[h, a * q + b]
            e["spread2"] = [link(own, own, device(s, a, step(b, d))) for d in range(1, q)]
            mine_lo = xb.at[h, grp(a), lo, :]
            mine_hi = xb.at[h, grp(a), hi, :]
            e["up"] = [link(mine_lo, mine_lo, to_up), link(mine_hi, mine_hi, to_up)]
            e["down"] = [link(mine_lo, mine_lo, to_down), link(mine_hi, mine_hi, to_down)]
            fwd_lo = xb.at[h, grp(down), lo, :]
            fwd_hi = xb.at[h, grp(up), hi, :]
            e["fwd"] = [link(fwd_lo, fwd_lo, to_up), link(fwd_hi, fwd_hi, to_down)]
            e["pass"] = [
                link(xb.at[h, grp(step(a, d))], xb.at[h, grp(step(a, d))], sibling)
                for d in range(q)
            ]
            plan["slots"].append(e)
        plans.append(plan)

    def mlp(k):
        off, rows = chunks[k]
        px = bufs[k][0]
        r2 = rows // 2
        loads[f"x{k}"].wait()
        wide = x_v[pl.ds(off, rows), :].astype(jnp.float32)
        normed = rms_rows(wide, scale_mlp)
        if k == 0:
            loads["wg"].wait()
            loads["wl"].wait()
        gate = jnp.dot(normed, wg_v[...], preferred_element_type=jnp.float32)
        lin = jnp.dot(normed, wl_v[...], preferred_element_type=jnp.float32)
        hidden = (jax.nn.gelu(gate, approximate=True) * lin).astype(jnp.bfloat16)
        if k == 0:
            loads["wo"].wait()
        part = jnp.dot(hidden, wo_v[...], preferred_element_type=jnp.float32)
        for h in range(2):
            for j in range(q * q):
                px[h, j] = part[h * r2:(h + 1) * r2, j * LANES:(j + 1) * LANES]

    def pair_send(k):
        def go():
            for l in plans[k]["pair"]:
                l.start()
        if NORTH:
            quiet(go)
        else:
            go()

    def first_send(k):
        px, dr = bufs[k][0], bufs[k][1]

        def go():
            for l in plans[k]["pair"]:
                l.came()
            for s in slots:
                a, _ = coords(s)
                h = half_of[s]
                e = plans[k]["slots"][s]
                for d in (2, 1, 3, 0):
                    g = pl.ds(step(a, d) * q, q)
                    dr[s, g] = dr[s, g] + px[h, g]
                    if d == 2:
                        for l in e["relay"]:
                            l.start()
                    if d == 3:
                        for l in e["direct"]:
                            l.start()
        talkers(go)

    def first_relay(k):
        _, dr, rl = bufs[k][:3]
        hr = chunks[k][1] // 4

        def go():
            for s in slots:
                a, _ = coords(s)
                e = plans[k]["slots"][s]
                for i, d in ((0, 1), (1, -1)):
                    e["relay"][i].came()
                    g = pl.ds(step(a, d) * q, q)
                    rl[s, i] = rl[s, i] + dr[s, g, i * hr:(i + 1) * hr, :]
                    e["comb"][i].start()
        talkers(go)

    def second_send(k):
        _, dr, _, dc, cb, bs = bufs[k][:6]
        hr = chunks[k][1] // 4

        def go():
            for s in slots:
                a, _ = coords(s)
                e = plans[k]["slots"][s]
                g = pl.ds(a * q, q)
                for i in range(2):
                    e["direct"][i].came()
                    e["comb"][i].came()
                    part = slice(i * hr, (i + 1) * hr)
                    bs[s, :, part, :] = dr[s, g, part, :] + dc[s, i] + cb[s, i]
                for l in e["second"]:
                    l.start()
        talkers(go)

    def own_block(k):
        off, rows = chunks[k]
        r2 = rows // 2
        bs, pr, xb = bufs[k][5:]

        def go():
            for s in slots:
                a, b = coords(s)
                h = half_of[s]
                e = plans[k]["slots"][s]
                for l in e["second"]:
                    l.came()
                total = bs[s, b]
                for d in range(q - 1):
                    total = total + pr[s, d]
                col = pl.ds(pl.multiple_of((a * q + b) * LANES, LANES), LANES)
                row = pl.ds(pl.multiple_of(off + h * r2, 16), r2)
                resid = x_v[row, col].astype(jnp.float32)
                xb[h, a * q + b] = (resid + total).astype(jnp.bfloat16).astype(jnp.float32)
                for l in e["spread2"]:
                    l.start()
        talkers(go)

    def spread_first(k):
        def go():
            for s in slots:
                e = plans[k]["slots"][s]
                for l in e["spread2"]:
                    l.came()
                e["up"][0].start()
                e["down"][1].start()
                e["up"][1].start()
                e["down"][0].start()
                e["pass"][0].start()
        talkers(go)

    def spread_forward(k):
        def go():
            for s in slots:
                e = plans[k]["slots"][s]
                e["up"][0].came()
                e["fwd"][0].start()
                e["down"][1].came()
                e["fwd"][1].start()
        talkers(go)

    def spread_last(k):
        def go():
            for s in slots:
                e = plans[k]["slots"][s]
                e["up"][1].came()
                e["pass"][q - 1].start()
                e["down"][0].came()
                e["pass"][1].start()
                for l in e["fwd"]:
                    l.came()
                e["pass"][2].start()
        talkers(go)

    def arrive(k):
        def go():
            for s in slots:
                for l in plans[k]["slots"][s]["pass"]:
                    l.came()
        if NORTH:
            quiet(go)
        else:
            go()

    def normalize(l):
        first = lm_chunks[l]
        base = chunks[first[0]][0]
        for k in first:
            off, rows = chunks[k]
            r2 = rows // 2
            xb = bufs[k][7]
            for h in range(2):
                sq = None
                for j in range(q * q):
                    v = xb[h, j]
                    sq = v * v if sq is None else sq + v * v
                mean_sq = jnp.sum(sq, axis=-1, keepdims=True) * (1.0 / (q * q * LANES))
                inv = jnp.broadcast_to(lax.rsqrt(mean_sq + EPS), (r2, LANES))
                for j in range(q * q):
                    cols = slice(j * LANES, (j + 1) * LANES)
                    z_v[off - base + h * r2:off - base + (h + 1) * r2, cols] = (
                        xb[h, j] * inv * scale_fin[:, cols]
                    ).astype(jnp.bfloat16)

    n_tiles = -(-vocab // TILE)

    def lm(l, t0, t1):
        rows = ROWS_LM
        base = chunks[lm_chunks[l][0]][0]
        loc = [ids_v[base:base + rows, c * LANES:(c + 1) * LANES] - me * vocab for c in range(2)]
        chunk = [jnp.where((v >= 0) & (v < vocab), lax.shift_right_arithmetic(v, 7), -1) for v in loc]
        lane = [v & (LANES - 1) for v in loc]
        if t0 == 0:
            top = total = None
            pick = [jnp.zeros((rows, LANES), jnp.float32) for _ in range(2)]
        else:
            top, total, pick = st_v[0], st_v[1], [st_v[2], st_v[3]]
        z = z_v[...]
        for t in range(t0, t1):
            a = t * TILE
            wd = min(TILE, vocab - a)
            slot = t % 2
            lg_v[slot, :, :wd] = jnp.dot(z, w_v[:, a:a + wd], preferred_element_type=jnp.float32)
            nv = -(-wd // LANES)
            xs = [lg_v[slot, :, j * LANES:(j + 1) * LANES] for j in range(nv)]
            if wd % LANES:
                pos = lax.broadcasted_iota(jnp.int32, (rows, LANES), 1)
                xs[-1] = jnp.where(pos < wd % LANES, xs[-1], NEG)
            peak = functools.reduce(jnp.maximum, xs)
            new = peak if top is None else jnp.maximum(top, peak)
            acc = None if total is None else total * jnp.exp(top - new)
            for v in xs:
                ev = jnp.exp(v - new)
                acc = ev if acc is None else acc + ev
            top, total = new, acc
            for c in range(2):
                for j in range(nv):
                    got = jnp.take_along_axis(xs[j], lane[c], axis=1, mode="promise_in_bounds")
                    pick[c] = jnp.where(chunk[c] == a // LANES + j, got, pick[c])
        if t1 < n_tiles:
            st_v[0], st_v[1], st_v[2], st_v[3] = top, total, pick[0], pick[1]
            return
        peak = jnp.max(top, axis=-1, keepdims=True)
        mass = jnp.sum(total * jnp.exp(top - peak), axis=-1, keepdims=True)
        part = jnp.broadcast_to(peak + jnp.log(mass), (rows, LANES))
        flat = part.T[0:8, :]
        tp = tails[l][0]
        r2 = rows // 2
        for h in range(2):
            for c in range(2):
                cols = slice(c * LANES, (c + 1) * LANES)
                tp[h, 0:r2, cols] = pick[c][h * r2:(h + 1) * r2, :]
                tp[h, r2:r2 + 8, cols] = flat

    r2 = ROWS_LM // 2
    tplans = []
    for l in range(len(lm_chunks)):
        tp, t1r, t2r, t3r, tc = tails[l]
        plan = {"slots": []}
        if NORTH:
            plan["pair"] = [link(tp.at[h], t1r.at[h], sibling, "quiet") for h in (0, 1)]
        else:
            plan["pair"] = [link(tp.at[1 - core], t1r.at[0], sibling)]
        for s in slots:
            a, b = coords(s)
            h = half_of[s]
            plan["slots"].append({
                "one": [link(t2r.at[s, a], t2r.at[s, a], device(s, step(a, d), b)) for d in range(1, q)],
                "two": [link(t3r.at[s, b], t3r.at[s, b], device(s, a, step(b, d))) for d in range(1, q)],
                "back": [link(tc.at[h], tc.at[h], sibling)],
            })
        tplans.append(plan)

    def join(refs, out):
        total = functools.reduce(jnp.add, [r[0:r2, :] for r in refs])
        out[0:r2, :] = total
        out[r2:r2 + 8, :] = log_add([r[r2:r2 + 8, :] for r in refs])

    def tail_pair(l):
        def go():
            for k in tplans[l]["pair"]:
                k.start()
        if NORTH:
            quiet(go)
        else:
            go()

    def tail_one(l):
        tp, t1r, t2r = tails[l][:3]

        def go():
            for k in tplans[l]["pair"]:
                k.came()
            for s in slots:
                join([tp.at[half_of[s]], t1r.at[s]], t2r.at[s, coords(s)[0]])
                for k in tplans[l]["slots"][s]["one"]:
                    k.start()
        talkers(go)

    def tail_two(l):
        t2r, t3r = tails[l][2:4]

        def go():
            for s in slots:
                for k in tplans[l]["slots"][s]["one"]:
                    k.came()
                join([t2r.at[s, d] for d in range(q)], t3r.at[s, coords(s)[1]])
                for k in tplans[l]["slots"][s]["two"]:
                    k.start()
        talkers(go)

    def tail_three(l):
        t3r, tc = tails[l][3:5]

        def go():
            for s in slots:
                for k in tplans[l]["slots"][s]["two"]:
                    k.came()
                join([t3r.at[s, d] for d in range(q)], tc.at[half_of[s]])
                for k in tplans[l]["slots"][s]["back"]:
                    k.start()
        talkers(go)

    outs = []

    def tail_done(l):
        tc = tails[l][4]

        def go():
            for s in slots:
                for k in tplans[l]["slots"][s]["back"]:
                    k.came()
        if NORTH:
            quiet(go)
        else:
            go()
        base = chunks[lm_chunks[l][0]][0]
        row = tc[0, r2:r2 + 1, 0:LANES]
        lnrow_v[l:l + 1, :] = row
        lse = jnp.broadcast_to(row, (LANES, LANES)).T
        for h in range(2):
            for c in range(2):
                cols = slice(c * LANES, (c + 1) * LANES)
                ob_v[base + h * r2:base + (h + 1) * r2, cols] = (
                    tc[h, 0:r2, cols] - lse[h * r2:(h + 1) * r2, :]
                )
        i = loc_count[0]
        loc_count[0] += 1
        cp = pltpu.make_async_copy(
            ob_v.at[base:base + ROWS_LM, :], lp_hbm.at[base:base + ROWS_LM, :], loc_sems.at[i])
        cp.start()
        outs.append(cp)

    stages = [mlp, pair_send, first_send, first_relay, second_send, own_block,
              spread_first, spread_forward, spread_last]
    names = {f.__name__: f for f in stages}
    names.update({f.__name__: f for f in (arrive, normalize, tail_pair, tail_one, tail_two, tail_three, tail_done)})
    for item in cfg["order"]:
        what, arg = item[0], item[1:]
        if what == "meet":
            meet()
        elif what == "weights":
            for i in range(parts):
                loads[f"w{i}"].wait()
        elif what == "ids":
            loads["ids"].wait()
        elif what == "lm":
            lm(*arg)
        else:
            names[what](*arg)

    i = loc_count[0]
    cp = pltpu.make_async_copy(lnrow_v, ln_hbm, loc_sems.at[i])
    cp.start()
    outs.append(cp)
    for cp in outs:
        cp.wait()

    def drain_talk():
        for l in started["talk"]:
            l.sent()

    talkers(drain_talk)

    def drain_quiet():
        for l in started["quiet"]:
            l.sent()

    quiet(drain_quiet)


def make_order(n, n_lm, lm_chunks, n_tiles):
    seq = ["first_send", "first_relay", "second_send", "own_block",
           "spread_first", "spread_forward", "spread_last", "arrive"]
    order = []
    todo = {k: list(seq) for k in range(n)}

    def advance(k):
        if todo[k]:
            order.append((todo[k].pop(0), k))

    for k in range(n):
        order.append(("mlp", k))
        if k == 0:
            order.append(("meet",))
        order.append(("pair_send", k))
        for j in range(k):
            advance(j)
    need = lm_chunks[0]
    while any(todo[k] for k in need):
        for k in range(n):
            advance(k)
            if not any(todo[j] for j in need):
                break
    tails = {}
    tseq = ["tail_one", "tail_two", "tail_three", "tail_done"]

    def service():
        for k in range(n):
            advance(k)
        for l in list(tails):
            if tails[l]:
                order.append((tails[l].pop(0), l))

    order.append(("ids",))
    order.append(("weights",))
    half = n_tiles // 2
    for l in range(n_lm):
        while any(todo[k] for k in lm_chunks[l]):
            for k in range(n):
                advance(k)
        order.append(("normalize", l))
        order.append(("lm", l, 0, half))
        service()
        order.append(("lm", l, half, n_tiles))
        order.append(("tail_pair", l))
        service()
        tails[l] = list(tseq)
    while any(tails.values()):
        for l in tails:
            if tails[l]:
                order.append((tails[l].pop(0), l))
    return order


def plan_chunks(batch):
    rows = ROWS_LM
    chunks = [(i * rows, rows) for i in range(batch // rows)]
    return chunks, [[i] for i in range(len(chunks))]


def solution(mesh):
    n_tp = mesh.shape["tp"]
    q = math.isqrt(n_tp // CORES)

    def local_step(resid_in, cand_ids, ln_mlp, wi_gate, wi_lin, w_out, ln_final, w_lm):
        batch, width = resid_in.shape
        inner = wi_gate.shape[1]
        vocab = w_lm.shape[1]
        cands = cand_ids.shape[1]
        chunks, lm_chunks = plan_chunks(batch)
        n_tiles = -(-vocab // TILE)
        w_parts = 4
        cfg = dict(q=q, chunks=chunks, lm=lm_chunks, w_parts=w_parts,
                   order=make_order(len(chunks), len(lm_chunks), lm_chunks, n_tiles))
        ns = 2 if NORTH else 1
        f32 = jnp.float32
        blocks = q * q
        bufs, tails = [], []
        for _, rows in chunks:
            r2 = rows // 2
            hr = r2 // 2
            bufs.append((
                pltpu.VMEM((2, blocks, r2, LANES), f32),
                pltpu.VMEM((ns, blocks, r2, LANES), f32),
                pltpu.VMEM((ns, 2, q, hr, LANES), f32),
                pltpu.VMEM((ns, 2, q, hr, LANES), f32),
                pltpu.VMEM((ns, 2, q, hr, LANES), f32),
                pltpu.VMEM((ns, q, r2, LANES), f32),
                pltpu.VMEM((ns, q - 1, r2, LANES), f32),
                pltpu.VMEM((2, blocks, r2, LANES), f32),
            ))
        rt = ROWS_LM // 2 + 8
        for _ in lm_chunks:
            tails.append((
                pltpu.VMEM((2, rt, cands), f32),
                pltpu.VMEM((ns, rt, cands), f32),
                pltpu.VMEM((ns, q, rt, cands), f32),
                pltpu.VMEM((ns, q, rt, cands), f32),
                pltpu.VMEM((2, rt, cands), f32),
            ))
        n_links = len(chunks) * (ns * 25 + 2) + len(lm_chunks) * (ns * 10 + 2)
        n_loc = len(chunks) + len(lm_chunks) + w_parts + 6
        hbm = pl.BlockSpec(memory_space=pltpu.HBM)
        vmem = pl.BlockSpec(memory_space=pltpu.VMEM)
        scratch = [
            pltpu.VMEM((batch, width), jnp.bfloat16),
            pltpu.VMEM((batch, cands), jnp.int32),
            pltpu.VMEM((width, inner), jnp.bfloat16),
            pltpu.VMEM((width, inner), jnp.bfloat16),
            pltpu.VMEM((inner, width), jnp.bfloat16),
            pltpu.VMEM((width, vocab), jnp.bfloat16),
            pltpu.VMEM((ROWS_LM, width), jnp.bfloat16),
            pltpu.VMEM((2, ROWS_LM, TILE), f32),
            pltpu.VMEM((4, ROWS_LM, LANES), f32),
            pltpu.VMEM((2, ROWS_LM // 2, LANES), f32),
            pltpu.VMEM((len(lm_chunks), LANES), f32),
            pltpu.VMEM((batch, cands), f32),
            tuple(bufs),
            tuple(tails),
            pltpu.SemaphoreType.DMA((n_links,)),
            pltpu.SemaphoreType.DMA((n_links,)),
            pltpu.SemaphoreType.DMA((n_loc,)),
        ]
        log_probs, log_norm = pl.pallas_call(
            functools.partial(fused, cfg),
            out_shape=(
                jax.ShapeDtypeStruct((batch, cands), f32),
                jax.ShapeDtypeStruct((len(lm_chunks), LANES), f32),
            ),
            in_specs=[hbm, hbm, vmem, hbm, hbm, hbm, vmem, hbm],
            out_specs=(hbm, hbm),
            scratch_shapes=scratch,
            compiler_params=pltpu.CompilerParams(
                collective_id=0, has_side_effects=True, vmem_limit_bytes=67_043_328),
            name="fused",
        )(resid_in, cand_ids, ln_mlp.reshape(1, width), wi_gate, wi_lin, w_out,
          ln_final.reshape(1, width), w_lm)
        return log_probs, log_norm.reshape(batch)

    in_specs = (P("dp", None), P("dp", None), P(None), P(None, "tp"), P(None, "tp"), P("tp", None), P(None), P(None, "tp"))
    return jax.shard_map(local_step, mesh=mesh, in_specs=in_specs, out_specs=(P("dp", None), P("dp")), check_vma=False)
```

time: 6080 us -> 154 us (0.03); the launches traced: 5980 us -> 153 us
  local copies, waits for them, and re-layouts: 3580 us -> 48.9 us
  blocking collectives: 2180 us -> 0 us
  waiting for transfers between devices: 144 us -> 0 us
  Pallas kernels: 0 us -> 103 us
    gather x2 -> x0, local copies, waits for them, and re-layouts: 3580 us -> none  [local_step(): jnp.take_along_axis(logits, jnp.clip(local_ids, 0, shard_cols - 1), axis=1)]
    psum x1 -> x0, blocking collectives: 2140 us -> none  [local_step(): lax.psum(jnp.sum(jnp.exp(logits - row_max[:, None]), axis=-1), 'tp')]
    psum x2 -> x0, waiting for transfers between devices: 144 us -> none  [the longest x1 105 us: local_step(): mlp_out = lax.psum(part_out, 'tp')]
    pallas_call x0 -> x1, Pallas kernels: none -> 103 us  [local_step(): pl.pallas_call(functools.partial(fused, cfg), out_shape=(jax.ShapeDtypeSt...]
  transfers between devices with their start and end apart: 2 -> 0, of which waited for: 2 -> 0; matrix products, arithmetic and copies ran while one was open for 0% -> 0% of each run, Pallas kernels for 0% -> 0%
where the time goes in v1:
time: 154 us; the launch traced here: 153 us
  Pallas kernels  103 us (67%)
  local copies, waits for them, and re-layouts  48.9 us (32%)
    pallas_call x1, Pallas kernels, local_step(): pl.pallas_call(functools.partial(fused, cfg), out_shape=(jax.ShapeDtypeSt...  103 us
    unnamed x5, local copies, waits for them, and re-layouts  46.3 us

profile of v1, /device:TPU:97, one launch (start us, length us, event | category | flops | bytes accessed | tf_op | source)
XLA Modules:
  0.0 152.8 jit_solution(11676392170532415233)
XLA Ops:
  0.6 1.3 reshape.13.lnm_ref
  1.9 1.3 reshape.14.lnf_ref
  3.2 2.2 %copy.10.wg_hbm = bf16[2048,160]{1,0:T(8,128)(2,1)} copy(bf16[2048,160]{0,1:T(8,128)(2,1)} %param.11) | data formatting | bytes 1310720 | tf_op args[3]
  5.4 2.2 %copy.11.wl_hbm = bf16[2048,160]{1,0:T(8,128)(2,1)} copy(bf16[2048,160]{0,1:T(8,128)(2,1)} %param.12) | data formatting | bytes 1310720 | tf_op args[4]
  7.6 38.9 %copy.12.w_hbm = bf16[2048,8012]{1,0:T(8,128)(2,1)} copy(bf16[2048,8012]{0,1:T(8,128)(2,1)} %param.15) | data formatting | bytes 65634304 | tf_op args[7]
  46.5 103.2 %fused.1 = (f32[512,256]{1,0:T(8,128)}, f32[4,128]{1,0:T(4,128)}) custom-call(bf16[512,2048]{1,0:T(8,128)(2,1)} %x_hbm.1, s32[512,256]{1,0:T(8,128)} %ids_hbm.1, bf16[1,2048]{1,0:T(2,128)(2,1)} %reshape.13.lnm_ref, bf16[2048,160]{1,0:T(8,128)(2,1)} %copy.10.wg_hbm, bf16[2048,160]{1,0:T(8,128)(2,1)} %copy.11.wl_hbm, bf16[160,2048]{1,0:T(8,128)(2,1)} %wo_hbm.1, ...), custom_call_target="tpu_custom_call" | custom-call | tf_op jit(solution)/shard_map/fused/pallas_call | solution.py:696
  149.7 1.9 %copy.15 = f32[512,256]{1,0:T(8,128)} copy(f32[512,256]{1,0:T(8,128)} %get-tuple-element.8) | data formatting | bytes 1048576
  151.6 1.2 copy.16
